TPU v7x, 128 devices: a whole 4x4x4 slice. The times are simulated.
128 devices in a mesh: row: 16 (over x, y), col: 8 (over z, core).
Axes of the slice: x: 4, y: 4, z: 4, core: 2. Of those that a mesh axis runs over, the one named last changes fastest.
Arguments:
- weights: int32 [8192, 8192], P('row', 'col'), may hold values from 1 to 64
Outputs:
- distances: int32 [8192, 8192], P('row', 'col')
All inputs are finite; a program needn't handle non-finite values.
Results may differ from a plain program's by a relative error of at most 0.000001.
Values may be sent and summed in bfloat16 or wider, within the bound.
A program may use at most 64 MiB of HBM per device.

v0:
```python
import jax
import jax.numpy as jnp
from jax import lax
from jax.sharding import PartitionSpec as P

PIVOT = 128
STEPS = 4


def broadcast(array, axis, root):
    return lax.dynamic_index_in_dim(lax.all_gather(array, axis), root, 0, keepdims=False)


def min_plus(acc, left, right):
    group = 8
    count = left.shape[1] // group

    def update(index, total):
        begin = (index * group).astype(jnp.int32)
        left_part = lax.dynamic_slice_in_dim(left, begin, group, 1)
        right_part = lax.dynamic_slice_in_dim(right, begin, group, 0)
        return jnp.minimum(total, jnp.min(left_part[:, :, None] + right_part[None, :, :], axis=1))

    return lax.fori_loop(0, count, update, acc)


def close_block(block):

    def relax(vertex, current):
        vertex = jnp.asarray(vertex).astype(jnp.int32)
        column = lax.dynamic_slice_in_dim(current, vertex, 1, 1)
        across = lax.dynamic_slice_in_dim(current, vertex, 1, 0)
        return jnp.minimum(current, column + across)

    return lax.fori_loop(0, block.shape[0], relax, block)


def per_device(weights):
    rows_dev, cols_dev = weights.shape
    verts = rows_dev * lax.axis_size("row")
    stride = verts // STEPS
    row_ids = lax.axis_index("row") * rows_dev + jnp.arange(rows_dev, dtype=jnp.int32)
    col_ids = lax.axis_index("col") * cols_dev + jnp.arange(cols_dev, dtype=jnp.int32)
    dist = jnp.where(row_ids[:, None] == col_ids[None, :], jnp.int32(0), weights).astype(jnp.int32)
    for step in range(STEPS):
        first = step * stride
        row_root = first // rows_dev
        row_off = first - row_root * rows_dev
        col_root = first // cols_dev
        col_off = first - col_root * cols_dev
        strip_rows = dist[row_off : row_off + PIVOT, :]
        strip_cols = dist[:, col_off : col_off + PIVOT]
        panel_rows = jax.tree.map(lambda part: broadcast(part, "row", row_root), strip_rows)
        closed = close_block(panel_rows[:, col_off : col_off + PIVOT])
        new_cols = min_plus(strip_cols, strip_cols, closed)
        panel_cols = jax.tree.map(lambda part: broadcast(part, "col", col_root), new_cols)
        dist = min_plus(dist, panel_cols, panel_rows)
    return dist


def solution(mesh):
    placed = (P("row", "col"),)
    return jax.shard_map(
        per_device, mesh=mesh, in_specs=placed, out_specs=P("row", "col"), check_vma=False
    )
```

profile of v0, /device:TPU:1, one launch (start us, length us, event | category | flops | bytes accessed | tf_op | source)
XLA Modules:
  0.0 1272.3 jit_solution(7129442671943326020)
XLA Ops:
  9.3 73.7 %all-gather.17.cloned.1.call-done = s32[2048,1024]{1,0:T(8,128)} async-done(((s32[128,1024]{1,0:T(8,128)}), s32[2048,1024]{1,0:T(8,128)}) %all-gather.17.cloned.1.call-update) | async-done | bytes 8388624 | tf_op jit(solution)/shard_map/all_gather | solution.py:11
  83.8 38.9 %while.156 = (s32[]{:T(128)}, s32[128,128]{1,0:T(8,128)S(1)}, s32[]{:T(128)}) while((s32[]{:T(128)}, s32[128,128]{1,0:T(8,128)S(1)}, s32[]{:T(128)}) %tuple.281), condition=%wide.region_1.2_spmd, body=%wide.region_0.1_spmd.sunk | while | flops 32770 | bytes 134205 | solution.py:35
  122.7 50.6 %while.157 = (s32[]{:T(128)}, s32[512,128]{1,0:T(8,128)S(1)}, s32[512,128]{1,0:T(8,128)S(1)}, s32[128,128]{1,0:T(8,128)S(1)}, s32[]{:T(128)}, /*index=5*/s32[]{:T(128)}, s32[]{:T(128)}, s32[]{:T(128)}) while((s32[]{:T(128)}, s32[512,128]{1,0:T(8,128)S(1)}, s32[512,128]{1,0:T(8,128)S(1)}, s32[128,128]{1,0:T(8,128)S(1)}, s32[]{:T(128)}, ...), condition=%wide.region_4.5_spmd, body=%wide.region_2.4_spmd.sunk | while | flops 1048582 | bytes 1110155 | solution.py:24
  174.1 26.0 %all-gather.19.cloned.1.call-done = s32[4096,128]{1,0:T(8,128)} async-done(((s32[512,128]{1,0:T(8,128)}), s32[4096,128]{1,0:T(8,128)}) %all-gather.19.cloned.1.call-update) | async-done | bytes 2097168 | tf_op jit(solution)/shard_map/all_gather | solution.py:11
  201.1 123.8 %while.158 = (s32[]{:T(128)}, s32[512,1024]{1,0:T(8,128)S(1)}, s32[512,128]{1,0:T(8,128)S(1)}, s32[128,1024]{1,0:T(8,128)S(1)}, s32[]{:T(128)}, /*index=5*/s32[]{:T(128)}, s32[]{:T(128)}, s32[]{:T(128)}) while((s32[]{:T(128)}, s32[512,1024]{1,0:T(8,128)S(1)}, s32[512,128]{1,0:T(8,128)S(1)}, s32[128,1024]{1,0:T(8,128)S(1)}, s32[]{:T(128)}, ...), condition=%wide.region_7.8_spmd, body=%wide.region_5.7_spmd.sunk | while | flops 8388614 | bytes 8536203 | solution.py:24
  201.3 6.9 add_reduce_fusion.17
  209.0 6.9 add_reduce_fusion.17
  216.8 6.9 add_reduce_fusion.17
  224.5 6.9 add_reduce_fusion.17
  232.2 6.9 add_reduce_fusion.17
  240.0 6.9 add_reduce_fusion.17
  247.7 6.9 add_reduce_fusion.17
  255.4 6.9 add_reduce_fusion.17
  301.9 6.9 add_reduce_fusion.17
  309.6 6.9 add_reduce_fusion.17
  317.3 6.9 add_reduce_fusion.17
  325.9 70.1 %all-gather.21.cloned.1.call-done = s32[2048,1024]{1,0:T(8,128)} async-done(((s32[128,1024]{1,0:T(8,128)}), s32[2048,1024]{1,0:T(8,128)}) %all-gather.21.cloned.1.call-update) | async-done | bytes 8388624 | tf_op jit(solution)/shard_map/all_gather | solution.py:11
  396.9 38.9 %while.159 = (s32[]{:T(128)}, s32[128,128]{1,0:T(8,128)S(1)}, s32[]{:T(128)}) while((s32[]{:T(128)}, s32[128,128]{1,0:T(8,128)S(1)}, s32[]{:T(128)}) %tuple.290), condition=%wide.region_9.10_spmd, body=%wide.region_8.9_spmd.sunk | while | flops 32770 | bytes 134205 | solution.py:35
  435.8 50.6 %while.160 = (s32[]{:T(128)}, s32[512,128]{1,0:T(8,128)S(1)}, s32[512,128]{1,0:T(8,128)S(1)}, s32[128,128]{1,0:T(8,128)S(1)}, s32[]{:T(128)}, /*index=5*/s32[]{:T(128)}, s32[]{:T(128)}, s32[]{:T(128)}) while((s32[]{:T(128)}, s32[512,128]{1,0:T(8,128)S(1)}, s32[512,128]{1,0:T(8,128)S(1)}, s32[128,128]{1,0:T(8,128)S(1)}, s32[]{:T(128)}, ...), condition=%wide.region_12.13_spmd, body=%wide.region_10.12_spmd.sunk | while | flops 1048582 | bytes 1110155 | solution.py:24
  487.2 26.0 %all-gather.23.cloned.1.call-done = s32[4096,128]{1,0:T(8,128)} async-done(((s32[512,128]{1,0:T(8,128)}), s32[4096,128]{1,0:T(8,128)}) %all-gather.23.cloned.1.call-update) | async-done | bytes 2097168 | tf_op jit(solution)/shard_map/all_gather | solution.py:11
  514.2 123.8 %while.161 = (s32[]{:T(128)}, s32[512,1024]{1,0:T(8,128)S(1)}, s32[512,128]{1,0:T(8,128)S(1)}, s32[128,1024]{1,0:T(8,128)S(1)}, s32[]{:T(128)}, /*index=5*/s32[]{:T(128)}, s32[]{:T(128)}, s32[]{:T(128)}) while((s32[]{:T(128)}, s32[512,1024]{1,0:T(8,128)S(1)}, s32[512,128]{1,0:T(8,128)S(1)}, s32[128,1024]{1,0:T(8,128)S(1)}, s32[]{:T(128)}, ...), condition=%wide.region_15.16_spmd, body=%wide.region_13.15_spmd.sunk | while | flops 8388614 | bytes 8536203 | solution.py:24
  529.8 6.9 add_reduce_fusion.19
  553.0 6.9 add_reduce_fusion.19
  576.3 6.9 add_reduce_fusion.19
  584.0 6.9 add_reduce_fusion.19
  607.2 6.9 add_reduce_fusion.19
  630.4 6.9 add_reduce_fusion.19
  639.0 70.1 %all-gather.25.cloned.1.call-done = s32[2048,1024]{1,0:T(8,128)} async-done(((s32[128,1024]{1,0:T(8,128)}), s32[2048,1024]{1,0:T(8,128)}) %all-gather.25.cloned.1.call-update) | async-done | bytes 8388624 | tf_op jit(solution)/shard_map/all_gather | solution.py:11
  710.0 38.9 %while.162 = (s32[]{:T(128)}, s32[128,128]{1,0:T(8,128)S(1)}, s32[]{:T(128)}) while((s32[]{:T(128)}, s32[128,128]{1,0:T(8,128)S(1)}, s32[]{:T(128)}) %tuple.299), condition=%wide.region_17.18_spmd, body=%wide.region_16.17_spmd.sunk | while | flops 32770 | bytes 134205 | solution.py:35
  748.9 50.6 %while.163 = (s32[]{:T(128)}, s32[512,128]{1,0:T(8,128)S(1)}, s32[512,128]{1,0:T(8,128)S(1)}, s32[128,128]{1,0:T(8,128)S(1)}, s32[]{:T(128)}, /*index=5*/s32[]{:T(128)}, s32[]{:T(128)}, s32[]{:T(128)}) while((s32[]{:T(128)}, s32[512,128]{1,0:T(8,128)S(1)}, s32[512,128]{1,0:T(8,128)S(1)}, s32[128,128]{1,0:T(8,128)S(1)}, s32[]{:T(128)}, ...), condition=%wide.region_20.21_spmd, body=%wide.region_18.20_spmd.sunk | while | flops 1048582 | bytes 1110155 | solution.py:24
  800.5 25.8 %all-gather.27.cloned.1.call-done = s32[4096,128]{1,0:T(8,128)} async-done(((s32[512,128]{1,0:T(8,128)}), s32[4096,128]{1,0:T(8,128)}) %all-gather.27.cloned.1.call-update) | async-done | bytes 2097168 | tf_op jit(solution)/shard_map/all_gather | solution.py:11
  827.3 123.8 %while.164 = (s32[]{:T(128)}, s32[512,1024]{1,0:T(8,128)S(1)}, s32[512,128]{1,0:T(8,128)S(1)}, s32[128,1024]{1,0:T(8,128)S(1)}, s32[]{:T(128)}, /*index=5*/s32[]{:T(128)}, s32[]{:T(128)}, s32[]{:T(128)}) while((s32[]{:T(128)}, s32[512,1024]{1,0:T(8,128)S(1)}, s32[512,128]{1,0:T(8,128)S(1)}, s32[128,1024]{1,0:T(8,128)S(1)}, s32[]{:T(128)}, ...), condition=%wide.region_23.24_spmd, body=%wide.region_21.23_spmd.sunk | while | flops 8388614 | bytes 8536203 | solution.py:24
  842.9 6.9 add_reduce_fusion.21
  866.1 6.9 add_reduce_fusion.21
  889.4 6.9 add_reduce_fusion.21
  912.6 6.9 add_reduce_fusion.21
  935.8 6.9 add_reduce_fusion.21
  952.1 70.1 %all-gather.29.cloned.1.call-done = s32[2048,1024]{1,0:T(8,128)} async-done(((s32[128,1024]{1,0:T(8,128)}), s32[2048,1024]{1,0:T(8,128)}) %all-gather.29.cloned.1.call-update) | async-done | bytes 8388624 | tf_op jit(solution)/shard_map/all_gather | solution.py:11
  1023.1 38.9 %while.165 = (s32[]{:T(128)}, s32[128,128]{1,0:T(8,128)S(1)}, s32[]{:T(128)}) while((s32[]{:T(128)}, s32[128,128]{1,0:T(8,128)S(1)}, s32[]{:T(128)}) %tuple.308), condition=%wide.region_25.26_spmd, body=%wide.region_24.25_spmd.sunk | while | flops 32770 | bytes 134205 | solution.py:35
  1062.0 50.6 %while.166 = (s32[]{:T(128)}, s32[512,128]{1,0:T(8,128)S(1)}, s32[512,128]{1,0:T(8,128)S(1)}, s32[128,128]{1,0:T(8,128)S(1)}, s32[]{:T(128)}, /*index=5*/s32[]{:T(128)}, s32[]{:T(128)}, s32[]{:T(128)}) while((s32[]{:T(128)}, s32[512,128]{1,0:T(8,128)S(1)}, s32[512,128]{1,0:T(8,128)S(1)}, s32[128,128]{1,0:T(8,128)S(1)}, s32[]{:T(128)}, ...), condition=%wide.region_28.29_spmd, body=%wide.region_26.28_spmd.sunk | while | flops 1048582 | bytes 1110155 | solution.py:24
  1113.3 26.1 %all-gather.31.cloned.1.call-done = s32[4096,128]{1,0:T(8,128)} async-done(((s32[512,128]{1,0:T(8,128)}), s32[4096,128]{1,0:T(8,128)}) %all-gather.31.cloned.1.call-update) | async-done | bytes 2097168 | tf_op jit(solution)/shard_map/all_gather | solution.py:11
  1140.4 123.8 %while.167 = (s32[]{:T(128)}, s32[512,1024]{1,0:T(8,128)S(1)}, s32[512,128]{1,0:T(8,128)S(1)}, s32[128,1024]{1,0:T(8,128)S(1)}, s32[]{:T(128)}, /*index=5*/s32[]{:T(128)}, s32[]{:T(128)}, s32[]{:T(128)}) while((s32[]{:T(128)}, s32[512,1024]{1,0:T(8,128)S(1)}, s32[512,128]{1,0:T(8,128)S(1)}, s32[128,1024]{1,0:T(8,128)S(1)}, s32[]{:T(128)}, ...), condition=%wide.region_31.32_spmd, body=%wide.region_29.31_spmd.sunk | while | flops 8388614 | bytes 8536203 | solution.py:24
  1140.5 6.9 add_reduce_fusion.23
  1156.0 6.9 add_reduce_fusion.23
  1194.7 6.9 add_reduce_fusion.23
  1210.2 6.9 add_reduce_fusion.23
  1233.4 6.9 add_reduce_fusion.23
  1248.9 6.9 add_reduce_fusion.23
  (2077 shorter events, 652.8 us)
Async XLA Ops:
  6.5 76.5 %all-gather.17.cloned.1.call-start = ((), (), s32[]{:S(2)}) async-start(), calls=%async_computation | async-start | bytes 8912896 | tf_op jit(solution)/shard_map/all_gather | solution.py:11
  9.2 190.9 %all-gather.19.cloned.1.call-start = ((), (), s32[]{:S(2)}) async-start(), calls=%async_computation.1 | async-start | bytes 2359296 | tf_op jit(solution)/shard_map/all_gather | solution.py:11
  122.7 78.4 %slice-start.1 = ((s32[2048,1024]{1,0:T(8,128)}), s32[128,1024]{1,0:T(8,128)S(1)}, s32[]{:S(2)}) async-start(s32[2048,1024]{1,0:T(8,128)} %all-gather.17.cloned.1.call-done), calls=%async_computation.9 | async-start | bytes 1048576 | tf_op jit(solution)/shard_map/jit(dynamic_index_in_dim)/dynamic_slice | solution.py:11
  173.4 0.7 copy-start.1
  174.1 222.0 %all-gather.21.cloned.1.call-start = ((), (), s32[]{:S(2)}) async-start(), calls=%async_computation.2 | async-start | bytes 8912896 | tf_op jit(solution)/shard_map/all_gather | solution.py:11
  325.8 187.4 %all-gather.23.cloned.1.call-start = ((), (), s32[]{:S(2)}) async-start(), calls=%async_computation.3 | async-start | bytes 2359296 | tf_op jit(solution)/shard_map/all_gather | solution.py:11
  435.8 78.4 %slice-start.2 = ((s32[2048,1024]{1,0:T(8,128)}), s32[128,1024]{1,0:T(8,128)S(1)}, s32[]{:S(2)}) async-start(s32[2048,1024]{1,0:T(8,128)} %all-gather.21.cloned.1.call-done), calls=%async_computation.10 | async-start | bytes 1048576 | tf_op jit(solution)/shard_map/jit(dynamic_index_in_dim)/dynamic_slice | solution.py:11
  486.4 0.7 copy-start.2
  487.1 222.0 %all-gather.25.cloned.1.call-start = ((), (), s32[]{:S(2)}) async-start(), calls=%async_computation.4 | async-start | bytes 8912896 | tf_op jit(solution)/shard_map/all_gather | solution.py:11
  638.9 187.4 %all-gather.27.cloned.1.call-start = ((), (), s32[]{:S(2)}) async-start(), calls=%async_computation.5 | async-start | bytes 2359296 | tf_op jit(solution)/shard_map/all_gather | solution.py:11
  748.8 78.4 %slice-start.3 = ((s32[2048,1024]{1,0:T(8,128)}), s32[128,1024]{1,0:T(8,128)S(1)}, s32[]{:S(2)}) async-start(s32[2048,1024]{1,0:T(8,128)} %all-gather.25.cloned.1.call-done), calls=%async_computation.11 | async-start | bytes 1048576 | tf_op jit(solution)/shard_map/jit(dynamic_index_in_dim)/dynamic_slice | solution.py:11
  799.5 0.7 copy-start.3
  800.2 222.0 %all-gather.29.cloned.1.call-start = ((), (), s32[]{:S(2)}) async-start(), calls=%async_computation.6 | async-start | bytes 8912896 | tf_op jit(solution)/shard_map/all_gather | solution.py:11
  952.0 187.4 %all-gather.31.cloned.1.call-start = ((), (), s32[]{:S(2)}) async-start(), calls=%async_computation.7 | async-start | bytes 2359296 | tf_op jit(solution)/shard_map/all_gather | solution.py:11
  1061.9 78.4 %slice-start = ((s32[2048,1024]{1,0:T(8,128)}), s32[128,1024]{1,0:T(8,128)S(1)}, s32[]{:S(2)}) async-start(s32[2048,1024]{1,0:T(8,128)} %all-gather.29.cloned.1.call-done), calls=%async_computation.8 | async-start | bytes 1048576 | tf_op jit(solution)/shard_map/jit(dynamic_index_in_dim)/dynamic_slice | solution.py:11
  1112.6 0.7 copy-start.4
  1264.2 1.3 copy-start
Sparse Core Ops, SparseCore 0:
  9.5 73.4 all-gather.16
  174.2 25.8 all-gather.18
  325.9 70.0 all-gather.20
  487.3 25.8 all-gather.22
  639.0 70.0 all-gather.24
  800.4 25.8 all-gather.26
  952.1 70.0 all-gather.28
  1113.4 25.8 all-gather.30
where the time goes:
time: 1270 us
  other arithmetic  719 us (57%)
  waiting for transfers between devices  388 us (31%)
  local copies, waits for them, and re-layouts  127 us (10%)
  loops' own time  24.3 us (2%)
  between operations  13.8 us (1%)
    reduce_min x128, other arithmetic, update(): jnp.min(left_part[:, :, None] + right_part[None, :, :], axis=1)  628 us
    all_gather x8, waiting for transfers between devices, broadcast(): lax.all_gather(array, axis)  388 us
    dynamic_slice x512, local copies, waits for them, and re-layouts, relax(): column = lax.dynamic_slice_in_dim(current, vertex, 1, 1)  88.4 us
    min x128, other arithmetic, update(): jnp.minimum(total, jnp.min(left_part[:, :, None] + right_part[None, :, :]...  45.4 us
    min x512, other arithmetic, relax(): return jnp.minimum(current, column + across)  43.1 us
  transfers between devices with their start and end apart: 8, of which 8 were waited for; matrix products, arithmetic and copies ran while one was open for 0% of the time, Pallas kernels for 0%

commit v1 on v0

v1 whole, which is shorter than its diff:
```python
import jax
import jax.numpy as jnp
from jax import lax
from jax.experimental import pallas as pl
from jax.experimental.pallas import tpu as pltpu
from jax.sharding import PartitionSpec as P

F32 = jnp.float32
BF16 = jnp.bfloat16
MESH = pl.DeviceIdType.MESH
ALPHA = 60.25
BETA = 6.2
SHIFT = 0.984
STEP = 2.0**-BETA
B = 128
S = 4


def encode(values):
    t = values.astype(F32) - 1.0
    half = jnp.floor(t * 0.5)
    odd = (t - 2.0 * half) > 0.5
    return jnp.exp2(ALPHA - BETA * half), odd


def enc_right(values):
    e, odd = encode(values)
    return jnp.where(odd, e * STEP, e).astype(BF16), e.astype(BF16)


def enc_left(values):
    e, odd = encode(values)
    first = lax.broadcasted_iota(jnp.int32, values.shape, 1) < B // 2
    odd_floor = jnp.where(odd, e, 0.0)
    even = jnp.where(odd, 0.0, e)
    odd_ceil = odd_floor * STEP
    pairs = []
    for keep in (first, jnp.logical_not(first)):
        of, ev, oc = (jnp.where(keep, u, 0.0).astype(BF16) for u in (odd_floor, even, odd_ceil))
        pairs.append((jnp.concatenate([of, ev], 1), jnp.concatenate([ev, oc], 1)))
    return pairs


def dot(left, right):
    return jnp.dot(left, right, preferred_element_type=F32)


def level(total):
    x = (2 * ALPHA / BETA + SHIFT) - jnp.log2(total) * (1.0 / BETA)
    return jnp.floor(jnp.minimum(x, 200.0))


def decode(floors, ceils):
    low = level(floors)
    return low + jnp.minimum(level(ceils), low + 1.0) + 2.0


def min_plus(left, right, old):
    (f0, c0), (f1, c1) = left
    floors = jnp.maximum(dot(f0, right), dot(f1, right))
    ceils = jnp.maximum(dot(c0, right), dot(c1, right))
    return jnp.minimum(old, decode(floors, ceils))


def remote(src, dst, send, recv, where):
    return pltpu.make_async_remote_copy(
        src_ref=src, dst_ref=dst, send_sem=send, recv_sem=recv, device_id=where, device_id_type=MESH
    )


def kernel(
    w_hbm, o_ref, w, yp, yi, rr, y, enc_row, enc_r,
    w_sem, pp_send, pp_recv, yp_send, yp_recv, yi_send, yi_recv, fp_send, fi_send,
    rs_send, rs_recv, rg_send, rg_recv,
):
    row, col = lax.axis_index("row"), lax.axis_index("col")
    cx, cy = row // S, row % S
    cz, core = col // 2, col % 2

    barrier = pltpu.get_barrier_semaphore()
    for d in range(1, 16):
        pl.semaphore_signal(barrier, inc=1, device_id={"row": (row + d) % 16}, device_id_type=MESH)
    for d in range(1, 8):
        pl.semaphore_signal(barrier, inc=1, device_id={"col": (col + d) % 8}, device_id_type=MESH)

    loads = [
        pltpu.make_async_copy(w_hbm.at[pl.ds(i * B, B)], w.at[pl.ds(i * B, B)], w_sem.at[i])
        for i in range(S)
    ]
    for load in loads:
        load.start()
    loads[0].wait()

    @pl.when(cy == 0)
    def _():
        for q in range(S):
            rr[cx, q] = w[q * 32 : (q + 1) * 32, :].astype(BF16)

    @pl.when(jnp.logical_and(cy == 0, core == 0))
    def _():
        yp[cz, cx] = w[0:B, 0:B].astype(BF16)

    for load in loads[1:]:
        load.wait()

    @pl.when(core == 0)
    def _():
        yi[cz] = w[:, 0:B].astype(BF16)

    pl.semaphore_wait(barrier, 22)

    def pp_copy(s, d):
        return remote(yp.at[cz, s], yp.at[cz, s], pp_send.at[d], pp_recv.at[s], {"row": (row + d) % 16})

    def scatter_copy(q):
        return remote(rr.at[cx, q], rr.at[cx, q], rs_send.at[q], rs_recv, {"row": cx * S + q})

    def gather_copy(d):
        return remote(
            rr.at[cx, cy], rr.at[cx, cy], rg_send.at[d], rg_recv.at[row], {"row": (row + d) % 16}
        )

    @pl.when(core == 0)
    def _():
        @pl.when(cy == 0)
        def _():
            for d in range(1, 16):
                pp_copy(cx, d).start()

        def own(buf, send, recv):
            for d in range(1, S):
                remote(
                    buf.at[cz], buf.at[cz], send.at[d], recv.at[cz], {"col": (cz + d) % S * 2}
                ).start()
            remote(buf.at[cz], buf.at[cz], send.at[0], recv.at[cz], {"col": col + 1}).start()

        def forward(buf, send, recv, fwd):
            for d in range(1, S):
                other = (cz + d) % S
                remote(buf.at[other], buf.at[other], send.at[0], recv.at[other], {"col": col + 1}).wait_recv()
                remote(buf.at[other], buf.at[other], fwd.at[d], recv.at[other], {"col": col + 1}).start()

        own(yi, yi_send, yi_recv)
        for s in range(S):
            @pl.when(jnp.logical_not(jnp.logical_and(cy == 0, cx == s)))
            def _():
                pp_copy(s, 1).wait_recv()
        own(yp, yp_send, yp_recv)

        @pl.when(cy == 0)
        def _():
            for q in range(1, S):
                scatter_copy(q).start()

        forward(yi, yi_send, yi_recv, fi_send)
        forward(yp, yp_send, yp_recv, fp_send)

    @pl.when(core == 1)
    def _():
        remote(yp.at[cz], yp.at[cz], yp_send.at[0], yp_recv.at[cz], {"col": col - 1}).wait_recv()

        @pl.when(cy == 0)
        def _():
            for q in range(1, S):
                scatter_copy(q).start()

        for buf, send, recv in ((yi, yi_send, yi_recv), (yp, yp_send, yp_recv)):
            for d in range(S):
                other = (cz + d) % S
                if d == 0 and buf is yp:
                    continue
                remote(buf.at[other], buf.at[other], send.at[0], recv.at[other], {"col": col - 1}).wait_recv()

    @pl.when(cy != 0)
    def _():
        remote(rr.at[cx, cy], rr.at[cx, cy], rs_send.at[0], rs_recv, {"row": cx * S}).wait_recv()

    for d in range(1, 16):
        @pl.when(jnp.logical_or(cy == 0, (row + d) % 16 != cx * S))
        def _():
            gather_copy(d).start()

    for t in range(S):
        for s in range(S):
            y[t, s * B : (s + 1) * B, :] = yp[t, s].astype(F32)
        y[t, S * B :, :] = yi[t].astype(F32)

    def close(s, _):
        r0 = pl.multiple_of(s * B, B)

        def square(_, block):
            return min_plus(enc_left(block), jnp.concatenate(enc_right(block), 0), block)

        block = lax.fori_loop(0, 6, square, y[s, pl.ds(r0, B), :])
        y[s, pl.ds(r0, B), :] = block
        closed = enc_left(block)

        def panel(t, _):
            old = y[t, pl.ds(r0, B), :]
            new = min_plus(closed, jnp.concatenate(enc_right(old), 0), old)
            y[t, pl.ds(r0, B), :] = new
            ceil, floor = enc_right(new)
            enc_row[t, 0:B, :] = ceil
            enc_row[t, B : 2 * B, :] = floor
            return 0

        lax.fori_loop(0, S, panel, 0)

        def rows(i, _):
            i0 = pl.multiple_of(i * B, B)
            left = enc_left(y[s, pl.ds(i0, B), :])
            for t in range(S):
                y[t, pl.ds(i0, B), :] = min_plus(left, enc_row[t], y[t, pl.ds(i0, B), :])
            return 0

        lax.fori_loop(s + 1, 2 * S, rows, 0)
        return 0

    lax.fori_loop(0, S, close, 0)

    for d in range(1, 16):
        other = (row + d) % 16
        ox, oy = other // S, other % S

        @pl.when(jnp.logical_not(jnp.logical_and(cy == 0, ox == cx)))
        def _():
            remote(
                rr.at[ox, oy], rr.at[ox, oy], rg_send.at[0], rg_recv.at[other], {"row": other}
            ).wait_recv()

    for s in range(S):
        for q in range(S):
            ceil, floor = enc_right(rr[s, q])
            enc_r[s, q * 32 : (q + 1) * 32, :] = ceil
            enc_r[s, B + q * 32 : B + (q + 1) * 32, :] = floor

    def product(i, _):
        i0 = pl.multiple_of(i * B, B)
        y0 = pl.multiple_of(S * B + i * B, B)
        lefts = [enc_left(y[s, pl.ds(y0, B), :]) for s in range(S)]

        def columns(j, _):
            j0 = pl.multiple_of(j * 256, 256)
            floors = ceils = None
            for s in range(S):
                right = enc_r[s, :, pl.ds(j0, 256)]
                for left_floor, left_ceil in lefts[s]:
                    df, dc = dot(left_floor, right), dot(left_ceil, right)
                    floors = df if floors is None else jnp.maximum(floors, df)
                    ceils = dc if ceils is None else jnp.maximum(ceils, dc)
            found = decode(floors, ceils).astype(jnp.int32)
            old = w[pl.ds(i0, B), pl.ds(j0, 256)]
            lag = lax.broadcasted_iota(jnp.int32, old.shape, 1) - lax.broadcasted_iota(jnp.int32, old.shape, 0)
            old = jnp.where(lag == row * 512 + i0 - col * 1024 - j0, 0, old)
            o_ref[pl.ds(i0, B), pl.ds(j0, 256)] = jnp.minimum(old, found)
            return 0

        lax.fori_loop(0, 4, columns, 0)
        return 0

    lax.fori_loop(0, 4, product, 0)

    @pl.when(core == 0)
    def _():
        @pl.when(cy == 0)
        def _():
            for d in range(1, 16):
                pp_copy(cx, d).wait_send()

        for buf, send, fwd, recv in ((yi, yi_send, fi_send, yi_recv), (yp, yp_send, fp_send, yp_recv)):
            for d in range(S):
                remote(buf.at[cz], buf.at[cz], send.at[d], recv.at[cz], {"col": col + 1}).wait_send()
            for d in range(1, S):
                other = (cz + d) % S
                remote(buf.at[other], buf.at[other], fwd.at[d], recv.at[other], {"col": col + 1}).wait_send()

    @pl.when(cy == 0)
    def _():
        for q in range(1, S):
            scatter_copy(q).wait_send()

    for d in range(1, 16):
        @pl.when(jnp.logical_or(cy == 0, (row + d) % 16 != cx * S))
        def _():
            gather_copy(d).wait_send()


def per_device(weights):
    dma = pltpu.SemaphoreType.DMA
    return pl.pallas_call(
        kernel,
        out_shape=jax.ShapeDtypeStruct(weights.shape, jnp.int32),
        in_specs=[pl.BlockSpec(memory_space=pl.ANY)],
        out_specs=pl.BlockSpec(memory_space=pltpu.VMEM),
        scratch_shapes=[
            pltpu.VMEM((512, 1024), jnp.int32),
            pltpu.VMEM((S, S, B, B), BF16),
            pltpu.VMEM((S, 512, B), BF16),
            pltpu.VMEM((S, S, 32, 1024), BF16),
            pltpu.VMEM((S, 1024, B), F32),
            pltpu.VMEM((S, 2 * B, B), BF16),
            pltpu.VMEM((S, 2 * B, 1024), BF16),
            dma((S,)), dma((16,)), dma((S,)), dma((S,)), dma((S,)), dma((S,)), dma((S,)), dma((S,)), dma((S,)),
            dma((S,)), dma, dma((16,)), dma((16,)),
        ],
        compiler_params=pltpu.CompilerParams(
            collective_id=0, has_side_effects=True, vmem_limit_bytes=56 * 2**20
        ),
        name="paths",
    )(weights)


def solution(mesh):
    return jax.shard_map(
        per_device, mesh=mesh, in_specs=(P("row", "col"),), out_specs=P("row", "col"), check_vma=False
    )
```

time: 1270 us -> 56.7 us (0.04)
  other arithmetic: 719 us -> 0 us
  waiting for transfers between devices: 388 us -> 0 us
  local copies, waits for them, and re-layouts: 127 us -> 3.16 us
  Pallas kernels: 0 us -> 53.4 us
  loops' own time: 24.3 us -> 0 us
  between operations: 13.8 us -> 0.01 us
    reduce_min x128 -> x0, other arithmetic: 628 us -> none  [update(): jnp.min(left_part[:, :, None] + right_part[None, :, :], axis=1)]
    all_gather x8 -> x0, waiting for transfers between devices: 388 us -> none  [broadcast(): lax.all_gather(array, axis)]
    dynamic_slice x780 -> x0, local copies, waits for them, and re-layouts: 110 us -> none  [the longest x512 88.4 us: relax(): column = lax.dynamic_slice_in_dim(current, vertex, 1, 1)]
    min x640 -> x0, other arithmetic: 88.5 us -> none  [the longest x128 45.4 us: update(): jnp.minimum(total, jnp.min(left_part[:, :, None] + right_part[None, :, :]...]
    pallas_call x0 -> x1, Pallas kernels: none -> 53.4 us  [per_device(): pl.pallas_call(kernel, out_shape=jax.ShapeDtypeStruct(weights.shape, jnp....]
    another operation x12 -> x0, loops' own time: 24.3 us -> none  [the longest x4 17.7 us: close_block(): return lax.fori_loop(0, block.shape[0], relax, block)]
  transfers between devices with their start and end apart: 8 -> 0, of which waited for: 8 -> 0; matrix products, arithmetic and copies ran while one was open for 0% -> 0% of each run, Pallas kernels for 0% -> 0%
where the time goes in v1:
time: 56.7 us; the launch traced here: 56.5 us
  Pallas kernels  53.4 us (94%)
  local copies, waits for them, and re-layouts  3.16 us (6%)
    pallas_call x1, Pallas kernels, per_device(): pl.pallas_call(kernel, out_shape=jax.ShapeDtypeStruct(weights.shape, jnp....  53.4 us
    unnamed x1, local copies, waits for them, and re-layouts  3.16 us

profile of v1, /device:TPU:1, one launch (start us, length us, event | category | flops | bytes accessed | tf_op | source)
XLA Modules:
  0.0 56.5 jit_solution(2646676050517628577)
XLA Ops:
  0.0 53.4 %paths.1 = s32[512,1024]{1,0:T(8,128)} custom-call(s32[512,1024]{1,0:T(8,128)} %w_hbm.1), custom_call_target="tpu_custom_call" | custom-call | tf_op jit(solution)/shard_map/paths/pallas_call | solution.py:290
  53.4 3.2 %copy.3 = s32[512,1024]{1,0:T(8,128)} copy(s32[512,1024]{1,0:T(8,128)} %paths.1) | data formatting | bytes 4194304

commit v2 on v0

v2 whole, which is shorter than its diff:
```python
import jax
import jax.numpy as jnp
from jax import lax
from jax.experimental import pallas as pl
from jax.experimental.pallas import tpu as pltpu
from jax.sharding import PartitionSpec as P

F32 = jnp.float32
BF16 = jnp.bfloat16
MESH = pl.DeviceIdType.MESH
ALPHA = 60.25
BETA = 6.2
SHIFT = 0.984
STEP = 2.0**-BETA
B = 128
S = 4


def encode(values):
    t = values.astype(F32) - 1.0
    half = jnp.floor(t * 0.5)
    odd = (t - 2.0 * half) > 0.5
    return jnp.exp2(ALPHA - BETA * half), odd


def enc_right(values):
    e, odd = encode(values)
    return jnp.where(odd, e * STEP, e).astype(BF16), e.astype(BF16)


def enc_left(values):
    e, odd = encode(values)
    first = lax.broadcasted_iota(jnp.int32, values.shape, 1) < B // 2
    odd_floor = jnp.where(odd, e, 0.0)
    even = jnp.where(odd, 0.0, e)
    odd_ceil = odd_floor * STEP
    pairs = []
    for keep in (first, jnp.logical_not(first)):
        of, ev, oc = (jnp.where(keep, u, 0.0).astype(BF16) for u in (odd_floor, even, odd_ceil))
        pairs.append((jnp.concatenate([of, ev], 1), jnp.concatenate([ev, oc], 1)))
    return pairs


def dot(left, right):
    return jnp.dot(left, right, preferred_element_type=F32)


def level(total):
    x = (2 * ALPHA / BETA + SHIFT) - jnp.log2(total) * (1.0 / BETA)
    return jnp.floor(jnp.minimum(x, 200.0))


def decode(floors, ceils):
    low = level(floors)
    return low + jnp.minimum(level(ceils), low + 1.0) + 2.0


def min_plus(left, right, old):
    (f0, c0), (f1, c1) = left
    floors = jnp.maximum(dot(f0, right), dot(f1, right))
    ceils = jnp.maximum(dot(c0, right), dot(c1, right))
    return jnp.minimum(old, decode(floors, ceils))


def remote(src, dst, send, recv, where):
    return pltpu.make_async_remote_copy(
        src_ref=src, dst_ref=dst, send_sem=send, recv_sem=recv, device_id=where, device_id_type=MESH
    )


def gather_kernel(
    w_hbm, x_ref, r0, r1, wp, wr, wc, rs, yp, yi, y, enc_row,
    w_sem, p1_send, p1_recv, p2_send, p2_recv, pf_send, yi_send, yi_recv, fi_send,
    s0_send, s0_recv, s1_send, s1_recv, a0_send, a0_recv, a1_send, a1_recv, b0_send, b0_recv, b1_send, b1_recv,
):
    row, col = lax.axis_index("row"), lax.axis_index("col")
    cx, cy = row // S, row % S
    cz, core = col // 2, col % 2
    block_owner = jnp.logical_and(cy == 0, core == 0)

    def at_x(x):
        return {"row": x * S + cy}

    def at_y(v):
        return {"row": cx * S + v}

    def in_slab(d):
        other = (cx * S + cz + d) % 16
        ox, oz = other // S, other % S
        return ox, oz, {"row": ox * S + cy, "col": oz * 2 + core}

    partner = {"col": cz * 2 + (1 - core)}

    barrier = pltpu.get_barrier_semaphore()

    def greet(where):
        pl.semaphore_signal(barrier, inc=1, device_id=where, device_id_type=MESH)

    for d in range(1, S):
        greet(at_y((cy + d) % S))
    for d in range(1, 16):
        greet(in_slab(d)[2])
    greet(partner)

    load_block = pltpu.make_async_copy(w_hbm.at[pl.ds(0, B), pl.ds(0, B)], wp, w_sem.at[0])
    load_rows = pltpu.make_async_copy(w_hbm.at[pl.ds(0, B)], wr, w_sem.at[1])
    load_cols = pltpu.make_async_copy(w_hbm.at[:, pl.ds(0, B)], wc, w_sem.at[2])

    @pl.when(block_owner)
    def _():
        load_block.start()

    @pl.when(cy == 0)
    def _():
        load_rows.start()

    @pl.when(core == 0)
    def _():
        load_cols.start()

    @pl.when(block_owner)
    def _():
        load_block.wait()
        yp[cz, cx] = wp[...].astype(BF16)

    @pl.when(core == 0)
    def _():
        load_cols.wait()
        yi[cz] = wc[...].astype(BF16)

    @pl.when(cy == 0)
    def _():
        load_rows.wait()
        for q in range(S):
            for h in range(2):
                rs[q, h] = wr[q * 32 : (q + 1) * 32, h * 512 : (h + 1) * 512].astype(BF16)
        r0[0, cx] = wr[0:32, 0:512].astype(BF16)
        r1[cx, 0] = wr[0:32, 512:1024].astype(BF16)

    pl.semaphore_wait(barrier, 19)

    def block_y(d):
        return remote(yp.at[cz, cx], yp.at[cz, cx], p1_send.at[d], p1_recv, at_y((cy + d) % S))

    def block_out(d, where):
        return remote(yp.at[cz, cx], yp.at[cz, cx], p2_send.at[d], p2_recv.at[cz * S + cx], where)

    def block_in(ox, oz, send, where):
        return remote(yp.at[oz, ox], yp.at[oz, ox], send, p2_recv.at[oz * S + ox], where)

    def cols_out(d, where):
        return remote(yi.at[cz], yi.at[cz], yi_send.at[d], yi_recv.at[cz], where)

    def cols_in(oz, send):
        return remote(yi.at[oz], yi.at[oz], send, yi_recv.at[oz], partner)

    def scatter(q):
        return (
            remote(rs.at[q, 0], r0.at[q, cx], s0_send.at[q], s0_recv, at_y(q)),
            remote(rs.at[q, 1], r1.at[cx, q], s1_send.at[q], s1_recv, at_y(q)),
        )

    def stage_a(d, x, v):
        return (
            remote(r0.at[cy, x], r0.at[cy, x], a0_send.at[d], a0_recv.at[x], at_x((cx + d) % S)),
            remote(r1.at[cx, v], r1.at[cx, v], a1_send.at[d], a1_recv.at[v], at_y((cy + d) % S)),
        )

    def stage_b(d, x, v):
        return (
            remote(r0.at[v], r0.at[v], b0_send.at[d], b0_recv.at[v], at_y((cy + d) % S)),
            remote(r1.at[x], r1.at[x], b1_send.at[d], b1_recv.at[x], at_x((cx + d) % S)),
        )

    def start_scatter():
        @pl.when(cy == 0)
        def _():
            for q in range(1, S):
                for copy in scatter(q):
                    copy.start()

    def start_a():
        @pl.when(cy != 0)
        def _():
            for copy in scatter(cy):
                copy.wait_recv()

        for d in range(1, S):
            for copy in stage_a(d, cx, cy):
                copy.start()

    def start_b():
        for d in range(1, S):
            for copy in stage_a(d, (cx + d) % S, (cy + d) % S):
                copy.wait_recv()
        for d in range(1, S):
            for copy in stage_b(d, cx, cy):
                copy.start()

    @pl.when(core == 0)
    def _():
        @pl.when(cy == 0)
        def _():
            for d in range(1, S):
                block_y(d).start()

        for d in range(1, S):
            cols_out(d, {"col": (cz + d) % S * 2}).start()
        cols_out(0, partner).start()
        start_scatter()

        @pl.when(cy != 0)
        def _():
            block_y(0).wait_recv()

        for d in range(1, 16):
            block_out(d, in_slab(d)[2]).start()
        block_out(0, partner).start()
        start_a()
        for d in range(1, S):
            oz = (cz + d) % S
            cols_in(oz, yi_send.at[0]).wait_recv()
            cols_in(oz, fi_send.at[d]).start()
        for d in range(1, 16):
            ox, oz, _ = in_slab(d)
            block_in(ox, oz, p2_send.at[0], partner).wait_recv()
            block_in(ox, oz, pf_send.at[d], partner).start()

    @pl.when(core == 1)
    def _():
        start_scatter()
        start_a()
        for oz in range(S):
            cols_in(oz, yi_send.at[0]).wait_recv()
        for d in range(16):
            ox, oz, _ = in_slab(d)
            block_in(ox, oz, p2_send.at[0], partner).wait_recv()

    start_b()

    for t in range(S):
        lanes = slice(t % 2 * B, (t % 2 + 1) * B)
        for s in range(S):
            y[t // 2, s * B : (s + 1) * B, lanes] = yp[t, s].astype(F32)
        y[t // 2, S * B :, lanes] = yi[t].astype(F32)

    def rows_of(i):
        return pl.ds(pl.multiple_of(i * B, B), B)

    def column(s, i):
        return y.at[s // 2, rows_of(i), pl.ds(pl.multiple_of(s % 2 * B, B), B)]

    def square(block):
        return min_plus(enc_left(block), jnp.concatenate(enc_right(block), 0), block)

    def update(s, i):
        left = enc_left(column(s, i)[...])
        for u in range(2):
            y[u, rows_of(i), :] = min_plus(left, enc_row[u], y[u, rows_of(i), :])

    def panel(s, block):
        column(s, s)[...] = block
        closed = enc_left(block)
        for u in range(2):
            old = y[u, rows_of(s), :]
            new = min_plus(closed, jnp.concatenate(enc_right(old), 0), old)
            y[u, rows_of(s), :] = new
            ceil, floor = enc_right(new)
            enc_row[u, 0:B, :] = ceil
            enc_row[u, B : 2 * B, :] = floor

    def close(s, block):
        panel(s, block)
        lax.fori_loop(s + 1, S, lambda i, _: update(s, i), None)

        def both(i, block):
            update(s, S + i)
            return square(block)

        block = lax.fori_loop(0, S, both, column(s + 1, s + 1)[...])
        return lax.fori_loop(0, 2, lambda _, block: square(block), block)

    block = lax.fori_loop(0, 6, lambda _, block: square(block), column(0, 0)[...])
    block = lax.fori_loop(0, S - 1, close, block)
    panel(S - 1, block)
    lax.fori_loop(S, 2 * S, lambda i, _: update(S - 1, i), None)
    for t in range(S):
        x_ref[t] = y[t // 2, S * B :, t % 2 * B : (t % 2 + 1) * B].astype(BF16)

    for d in range(1, S):
      for copy in stage_b(d, (cx + d) % S, (cy + d) % S):
          copy.wait_recv()

    @pl.when(core == 0)
    def _():
        @pl.when(cy == 0)
        def _():
            for d in range(1, S):
                block_y(d).wait_send()

        for d in range(16):
            block_out(d, partner).wait_send()
        for d in range(S):
            cols_out(d, partner).wait_send()
        for d in range(1, S):
            cols_in((cz + d) % S, fi_send.at[d]).wait_send()
        for d in range(1, 16):
            ox, oz, _ = in_slab(d)
            block_in(ox, oz, pf_send.at[d], partner).wait_send()

    @pl.when(cy == 0)
    def _():
      for q in range(1, S):
          for copy in scatter(q):
              copy.wait_send()

    for d in range(1, S):
      for copy in stage_a(d, cx, cy):
          copy.wait_send()
    for d in range(1, S):
      for copy in stage_b(d, cx, cy):
          copy.wait_send()


def product_kernel(w_ref, x_ref, r0, r1, o_ref, enc_r):
    i = pl.program_id(0)
    row, col = lax.axis_index("row"), lax.axis_index("col")

    @pl.when(i == 0)
    def _():
        def encode_strip(s, _):
            for q in range(S):
                for h, part in ((0, r0[q, s]), (1, r1[s, q])):
                    ceil, floor = enc_right(part)
                    enc_r[s, q * 32 : (q + 1) * 32, h * 512 : (h + 1) * 512] = ceil
                    enc_r[s, B + q * 32 : B + (q + 1) * 32, h * 512 : (h + 1) * 512] = floor
            return 0

        lax.fori_loop(0, S, encode_strip, 0)

    lefts = [enc_left(x_ref[s]) for s in range(S)]

    def columns(j, _):
        j0 = pl.multiple_of(j * 256, 256)
        floors = ceils = None
        for s in range(S):
            right = enc_r[s, :, pl.ds(j0, 256)]
            for left_floor, left_ceil in lefts[s]:
                df, dc = dot(left_floor, right), dot(left_ceil, right)
                floors = df if floors is None else jnp.maximum(floors, df)
                ceils = dc if ceils is None else jnp.maximum(ceils, dc)
        found = decode(floors, ceils).astype(jnp.int32)
        old = w_ref[:, pl.ds(j0, 256)]
        lag = lax.broadcasted_iota(jnp.int32, old.shape, 1) - lax.broadcasted_iota(jnp.int32, old.shape, 0)
        old = jnp.where(lag == row * 512 + i * B - col * 1024 - j0, 0, old)
        o_ref[:, pl.ds(j0, 256)] = jnp.minimum(old, found)
        return 0

    lax.fori_loop(0, 4, columns, 0)


def per_device(weights):
    dma = pltpu.SemaphoreType.DMA
    vmem = pl.BlockSpec(memory_space=pltpu.VMEM)
    rows, cols = weights.shape
    closed, r0, r1 = pl.pallas_call(
        gather_kernel,
        out_shape=(
            jax.ShapeDtypeStruct((S, rows, B), BF16),
            jax.ShapeDtypeStruct((S, S, 32, 512), BF16),
            jax.ShapeDtypeStruct((S, S, 32, 512), BF16),
        ),
        in_specs=[pl.BlockSpec(memory_space=pltpu.HBM)],
        out_specs=(vmem, vmem, vmem),
        scratch_shapes=[
            pltpu.VMEM((B, B), jnp.int32),
            pltpu.VMEM((B, cols), jnp.int32),
            pltpu.VMEM((rows, B), jnp.int32),
            pltpu.VMEM((S, 2, 32, 512), BF16),
            pltpu.VMEM((S, S, B, B), BF16),
            pltpu.VMEM((S, rows, B), BF16),
            pltpu.VMEM((2, 1024, 2 * B), F32),
            pltpu.VMEM((2, 2 * B, 2 * B), BF16),
            dma((3,)), dma((S,)), dma, dma((16,)), dma((16,)), dma((16,)), dma((S,)), dma((S,)), dma((S,)),
            dma((S,)), dma, dma((S,)), dma,
            dma((S,)), dma((S,)), dma((S,)), dma((S,)), dma((S,)), dma((S,)), dma((S,)), dma((S,)),
        ],
        compiler_params=pltpu.CompilerParams(
            collective_id=0, has_side_effects=True, vmem_limit_bytes=24 * 2**20
        ),
        name="gather",
    )(weights)
    return pl.pallas_call(
        product_kernel,
        grid=(S,),
        out_shape=jax.ShapeDtypeStruct(weights.shape, jnp.int32),
        in_specs=[
            pl.BlockSpec((B, cols), lambda i: (i, 0)),
            pl.BlockSpec((S, B, B), lambda i: (0, i, 0)),
            vmem,
            vmem,
        ],
        out_specs=pl.BlockSpec((B, cols), lambda i: (i, 0)),
        scratch_shapes=[pltpu.VMEM((S, 2 * B, cols), BF16)],
        compiler_params=pltpu.CompilerParams(vmem_limit_bytes=24 * 2**20),
        name="product",
    )(weights, closed, r0, r1)


def solution(mesh):
    return jax.shard_map(
        per_device, mesh=mesh, in_specs=(P("row", "col"),), out_specs=P("row", "col"), check_vma=False
    )
```

time: 1270 us -> 45.2 us (0.04)
  other arithmetic: 719 us -> 0 us
  waiting for transfers between devices: 388 us -> 0 us
  local copies, waits for them, and re-layouts: 127 us -> 1.59 us
  Pallas kernels: 0 us -> 43.3 us
  loops' own time: 24.3 us -> 0 us
  between operations: 13.8 us -> 0.01 us
    reduce_min x128 -> x0, other arithmetic: 628 us -> none  [update(): jnp.min(left_part[:, :, None] + right_part[None, :, :], axis=1)]
    all_gather x8 -> x0, waiting for transfers between devices: 388 us -> none  [broadcast(): lax.all_gather(array, axis)]
    dynamic_slice x780 -> x0, local copies, waits for them, and re-layouts: 110 us -> none  [the longest x512 88.4 us: relax(): column = lax.dynamic_slice_in_dim(current, vertex, 1, 1)]
    min x640 -> x0, other arithmetic: 88.5 us -> none  [the longest x128 45.4 us: update(): jnp.minimum(total, jnp.min(left_part[:, :, None] + right_part[None, :, :]...]
    pallas_call x0 -> x2, Pallas kernels: none -> 43.3 us  [the longest x1 32.3 us: per_device(): pl.pallas_call(gather_kernel, out_shape=(jax.ShapeDtypeStruct((S, rows, B...]
    another operation x12 -> x0, loops' own time: 24.3 us -> none  [the longest x4 17.7 us: close_block(): return lax.fori_loop(0, block.shape[0], relax, block)]
  transfers between devices with their start and end apart: 8 -> 0, of which waited for: 8 -> 0; matrix products, arithmetic and copies ran while one was open for 0% -> 0% of each run, Pallas kernels for 0% -> 0%
where the time goes in v2:
time: 45.2 us; the launch traced here: 44.9 us
  Pallas kernels  43.3 us (96%)
  local copies, waits for them, and re-layouts  1.59 us (4%)
    pallas_call x1, Pallas kernels, per_device(): pl.pallas_call(gather_kernel, out_shape=(jax.ShapeDtypeStruct((S, rows, B...  32.3 us
    pallas_call x1, Pallas kernels, per_device(): pl.pallas_call(product_kernel, grid=(S,), out_shape=jax.ShapeDtypeStruct(...  11 us
    unnamed x2, local copies, waits for them, and re-layouts  1.59 us

profile of v2, /device:TPU:1, one launch (start us, length us, event | category | flops | bytes accessed | tf_op | source)
XLA Modules:
  0.0 44.9 jit_solution(11909625899665949175)
XLA Ops:
  0.0 0.0 copy-start
  0.0 1.6 %copy-done = s32[512,1024]{1,0:T(8,128)S(1)} copy-done((s32[512,1024]{1,0:T(8,128)S(1)}, s32[512,1024]{1,0:T(8,128)}, u32[]{:S(2)}) %copy-start) | copy-done | bytes 2097176
  1.6 32.3 %gather.1 = (bf16[4,512,128]{2,1,0:T(8,128)(2,1)S(1)}, bf16[4,4,32,512]{3,2,1,0:T(8,128)(2,1)S(1)}, bf16[4,4,32,512]{3,2,1,0:T(8,128)(2,1)S(1)}) custom-call(s32[512,1024]{1,0:T(8,128)S(1)} %copy-done), custom_call_target="tpu_custom_call" | custom-call | tf_op jit(solution)/shard_map/gather/pallas_call | solution.py:366
  33.9 11.0 %product.1 = s32[512,1024]{1,0:T(8,128)} custom-call(s32[512,1024]{1,0:T(8,128)S(1)} %copy-done, bf16[4,512,128]{2,1,0:T(8,128)(2,1)S(1)} %get-tuple-element.8.x_ref, bf16[4,4,32,512]{3,2,1,0:T(8,128)(2,1)S(1)} %get-tuple-element.9.r0, bf16[4,4,32,512]{3,2,1,0:T(8,128)(2,1)S(1)} %get-tuple-element.10.r1), custom_call_target="tpu_custom_call" | custom-call | tf_op jit(solution)/shard_map/product/pallas_call | solution.py:393
Async XLA Ops:
  0.0 1.6 %copy-start = (s32[512,1024]{1,0:T(8,128)S(1)}, s32[512,1024]{1,0:T(8,128)}, u32[]{:S(2)}) copy-start(s32[512,1024]{1,0:T(8,128)} %w_ref.1) | copy-start | bytes 6291460

commit v3 on v2

v3 whole, which is shorter than its diff:
```python
import math

import jax
import jax.numpy as jnp
from jax import lax
from jax.experimental import pallas as pl
from jax.experimental.pallas import tpu as pltpu
from jax.sharding import PartitionSpec as P

F32 = jnp.float32
BF16 = jnp.bfloat16
MESH = pl.DeviceIdType.MESH
ALPHA = 60.25
BETA = 6.2
SHIFT = 0.984
STEP = 2.0**-BETA
B = 128
S = 4


LOG = 1.0 / (BETA * math.log(2.0))
FLOOR = 2 * ALPHA / BETA + SHIFT


def encode(t):
    u = t * 0.5
    half = jnp.floor(u)
    return jnp.exp2(half * -BETA + ALPHA), u > half


def enc_right(t):
    e, odd = encode(t)
    return jnp.where(odd, e * STEP, e).astype(BF16), e.astype(BF16)


def split_left(t):
    e, odd = encode(t)
    odd_floor = jnp.where(odd, e, 0.0)
    return tuple(u.astype(BF16) for u in (odd_floor, jnp.where(odd, 0.0, e), odd_floor * STEP))


def enc_left(t):
    first = jnp.where(lax.broadcasted_iota(jnp.int32, t.shape, 1) < B // 2, 1.0, 0.0)
    pairs = []
    parts = split_left(t)
    for keep in (first.astype(BF16), (1.0 - first).astype(BF16)):
        of, ev, oc = (u * keep for u in parts)
        pairs.append((jnp.concatenate([of, ev], 1), jnp.concatenate([ev, oc], 1)))
    return pairs


def dot(left, right):
    return jnp.dot(left, right, preferred_element_type=F32)


def decode(floors, ceils, bias):
    low = jnp.floor(FLOOR - jnp.log(floors) * LOG)
    high = jnp.floor(FLOOR + bias - jnp.log(ceils) * LOG)
    return low + jnp.minimum(high, low + (1.0 + bias))


def min_plus(left, right, old):
    (f0, c0), (f1, c1) = left
    floors = jnp.maximum(dot(f0, right), dot(f1, right))
    ceils = jnp.maximum(dot(c0, right), dot(c1, right))
    return jnp.minimum(old, decode(floors, ceils, 1.0))


def min_plus_block(block):
    of, ev, oc = split_left(block)
    ceil, floor = enc_right(block)
    none = jnp.zeros((B // 2, B), BF16)
    first = jnp.concatenate([ceil[: B // 2], none, floor[: B // 2], none], 0)
    second = jnp.concatenate([none, ceil[B // 2 :], none, floor[B // 2 :]], 0)
    right = jnp.concatenate([first, second], 1)
    floors = dot(jnp.concatenate([of, ev], 1), right)
    ceils = dot(jnp.concatenate([ev, oc], 1), right)
    floors = jnp.maximum(floors[:, :B], floors[:, B:])
    ceils = jnp.maximum(ceils[:, :B], ceils[:, B:])
    return jnp.minimum(block, decode(floors, ceils, 1.0))


def remote(src, dst, send, recv, where):
    return pltpu.make_async_remote_copy(
        src_ref=src, dst_ref=dst, send_sem=send, recv_sem=recv, device_id=where, device_id_type=MESH
    )


def gather_kernel(
    w, x_ref, r0, r1, rs, yp, yi, y, enc_row,
    p1_send, p1_recv, p2_send, p2_recv, pf_send, yi_send, yi_recv, fi_send,
    s0_send, s0_recv, s1_send, s1_recv, a0_send, a0_recv, a1_send, a1_recv, b0_send, b0_recv, b1_send, b1_recv,
):
    row, col = lax.axis_index("row"), lax.axis_index("col")
    cx, cy = row // S, row % S
    cz, core = col // 2, col % 2
    block_owner = jnp.logical_and(cy == 0, core == 0)

    def at_x(x):
        return {"row": x * S + cy}

    def at_y(v):
        return {"row": cx * S + v}

    def in_slab(d):
        other = (cx * S + cz + d) % 16
        ox, oz = other // S, other % S
        return ox, oz, {"row": ox * S + cy, "col": oz * 2 + core}

    partner = {"col": cz * 2 + (1 - core)}

    barrier = pltpu.get_barrier_semaphore()

    def greet(where):
        pl.semaphore_signal(barrier, inc=1, device_id=where, device_id_type=MESH)

    for d in range(1, S):
        greet(at_y((cy + d) % S))
    for d in range(1, 16):
        greet(in_slab(d)[2])
    greet(partner)

    @pl.when(block_owner)
    def _():
        yp[cz, cx] = w[0:B, 0:B].astype(BF16)

    @pl.when(core == 0)
    def _():
        yi[cz] = w[:, 0:B].astype(BF16)

    @pl.when(cy == 0)
    def _():
        for q in range(S):
            for h in range(2):
                rs[q, h] = w[q * 32 : (q + 1) * 32, h * 512 : (h + 1) * 512].astype(BF16)
        r0[0, cx] = w[0:32, 0:512].astype(BF16)
        r1[cx, 0] = w[0:32, 512:1024].astype(BF16)

    pl.semaphore_wait(barrier, 19)

    def block_y(d):
        return remote(yp.at[cz, cx], yp.at[cz, cx], p1_send.at[d], p1_recv, at_y((cy + d) % S))

    def block_out(d, where):
        return remote(yp.at[cz, cx], yp.at[cz, cx], p2_send.at[d], p2_recv.at[cz * S + cx], where)

    def block_in(ox, oz, send, where):
        return remote(yp.at[oz, ox], yp.at[oz, ox], send, p2_recv.at[oz * S + ox], where)

    def cols_out(d, where):
        return remote(yi.at[cz], yi.at[cz], yi_send.at[d], yi_recv.at[cz], where)

    def cols_in(oz, send):
        return remote(yi.at[oz], yi.at[oz], send, yi_recv.at[oz], partner)

    def scatter(q):
        return (
            remote(rs.at[q, 0], r0.at[q, cx], s0_send.at[q], s0_recv, at_y(q)),
            remote(rs.at[q, 1], r1.at[cx, q], s1_send.at[q], s1_recv, at_y(q)),
        )

    def stage_a(d, x, v):
        return (
            remote(r0.at[cy, x], r0.at[cy, x], a0_send.at[d], a0_recv.at[x], at_x((cx + d) % S)),
            remote(r1.at[cx, v], r1.at[cx, v], a1_send.at[d], a1_recv.at[v], at_y((cy + d) % S)),
        )

    def stage_b(d, x, v):
        return (
            remote(r0.at[v], r0.at[v], b0_send.at[d], b0_recv.at[v], at_y((cy + d) % S)),
            remote(r1.at[x], r1.at[x], b1_send.at[d], b1_recv.at[x], at_x((cx + d) % S)),
        )

    def start_scatter():
        @pl.when(cy == 0)
        def _():
            for q in range(1, S):
                for copy in scatter(q):
                    copy.start()

    def start_a():
        @pl.when(cy != 0)
        def _():
            for copy in scatter(cy):
                copy.wait_recv()

        for d in range(1, S):
            for copy in stage_a(d, cx, cy):
                copy.start()

    def start_b():
        for d in range(1, S):
            for copy in stage_a(d, (cx + d) % S, (cy + d) % S):
                copy.wait_recv()
        for d in range(1, S):
            for copy in stage_b(d, cx, cy):
                copy.start()

    @pl.when(block_owner)
    def _():
        for d in range(1, S):
            block_y(d).start()

    @pl.when(core == 0)
    def _():
        for d in range(1, S):
            cols_out(d, {"col": (cz + d) % S * 2}).start()
        cols_out(0, partner).start()
        start_scatter()

        @pl.when(cy != 0)
        def _():
            block_y(0).wait_recv()

        for d in range(1, 16):
            block_out(d, in_slab(d)[2]).start()
        block_out(0, partner).start()
        start_a()
        for d in range(1, S):
            oz = (cz + d) % S
            cols_in(oz, yi_send.at[0]).wait_recv()
            cols_in(oz, fi_send.at[d]).start()

    @pl.when(core == 1)
    def _():
        start_scatter()
        start_a()
        for oz in range(S):
            cols_in(oz, yi_send.at[0]).wait_recv()
        block_in(cx, cz, p2_send.at[0], partner).wait_recv()

    here = cx * S + cz

    def take(d):
        ox, oz, _ = in_slab(d)
        block_in(ox, oz, p2_send.at[0], partner).wait_recv()

        @pl.when(core == 0)
        def _():
            block_in(ox, oz, pf_send.at[d], partner).start()

    def take_other(d):
        @pl.when((here + d) % 16 != 0)
        def _():
            take(d)

    def rows_of(i):
        return pl.ds(i * B, B)

    def column(s, i):
        return y.at[s // 2, rows_of(i), pl.ds(s % 2 * B, B)]

    def update(s, i, which=(0, 1)):
        left = enc_left(column(s, i)[...])
        for u in which:
            y[u, rows_of(i), :] = min_plus(left, enc_row[s % 2, u], y[u, rows_of(i), :])

    def panel(s, block):
        column(s, s)[...] = block
        closed = enc_left(block)
        for u in range(2):
            old = y[u, rows_of(s), :]
            new = min_plus(closed, jnp.concatenate(enc_right(old), 0), old)
            y[u, rows_of(s), :] = new
            ceil, floor = enc_right(new)
            enc_row[s % 2, u, 0:B, :] = ceil
            enc_row[s % 2, u, B : 2 * B, :] = floor

    @pl.when(here != 0)
    def _():
        take((16 - here) % 16)

    def square_and_take(i, block):
        block = min_plus_block(block)
        for d in range(3):
            take_other(1 + 3 * i + d)
        return block

    block = lax.fori_loop(0, 5, square_and_take, yp[0, 0].astype(F32) - 1.0)
    start_b()
    block = min_plus_block(block)

    for t in range(S):
        lanes = slice(t % 2 * B, (t % 2 + 1) * B)
        for s in range(S):
            y[t // 2, s * B : (s + 1) * B, lanes] = yp[t, s].astype(F32) - 1.0
        y[t // 2, S * B :, lanes] = yi[t].astype(F32) - 1.0

    for s in range(S - 1):
        panel(s, block)
        near = (s + 1) // 2
        update(s, s + 1, (near,))
        block = column(s + 1, s + 1)[...]
        rest = [(s + 1, (1 - near,))] + [(i, (0, 1)) for i in range(s + 2, 2 * S)]
        done = 0
        for q in range(6):
            block = min_plus_block(block)
            until = -(-len(rest) * (q + 1) // 6)
            for i, which in rest[done:until]:
                update(s, i, which)
            done = until
    panel(S - 1, block)
    for i in range(S, 2 * S):
        update(S - 1, i)
    for t in range(S):
        x_ref[t] = y[t // 2, S * B :, t % 2 * B : (t % 2 + 1) * B].astype(BF16)

    for d in range(1, S):
        for copy in stage_b(d, (cx + d) % S, (cy + d) % S):
            copy.wait_recv()

    @pl.when(core == 0)
    def _():
        @pl.when(cy == 0)
        def _():
            for d in range(1, S):
                block_y(d).wait_send()

        for d in range(16):
            block_out(d, partner).wait_send()
        for d in range(S):
            cols_out(d, partner).wait_send()
        for d in range(1, S):
            cols_in((cz + d) % S, fi_send.at[d]).wait_send()
        for d in range(1, 16):
            ox, oz, _ = in_slab(d)
            block_in(ox, oz, pf_send.at[d], partner).wait_send()

    @pl.when(cy == 0)
    def _():
      for q in range(1, S):
          for copy in scatter(q):
              copy.wait_send()

    for d in range(1, S):
      for copy in stage_a(d, cx, cy):
          copy.wait_send()
    for d in range(1, S):
      for copy in stage_b(d, cx, cy):
          copy.wait_send()


def product_kernel(w, x_ref, r0, r1, o_hbm, o, enc_r, o_sem):
    row, col = lax.axis_index("row"), lax.axis_index("col")
    wide = 2 * B
    parts = [pl.ds(j * wide, wide) for j in range(w.shape[1] // wide)]
    stores = [pltpu.make_async_copy(o.at[:, p], o_hbm.at[:, p], o_sem.at[j]) for j, p in enumerate(parts)]

    def encode_strip(s, _):
        for q in range(S):
            for h, part in ((0, r0[q, s]), (1, r1[s, q])):
                ceil, floor = enc_right(part.astype(F32) - 1.0)
                enc_r[s, q * 32 : (q + 1) * 32, h * 512 : (h + 1) * 512] = ceil
                enc_r[s, B + q * 32 : B + (q + 1) * 32, h * 512 : (h + 1) * 512] = floor
        return 0

    lax.fori_loop(0, S, encode_strip, 0)
    lefts = [enc_left(x_ref[s].astype(F32)) for s in range(S)]
    for j, p in enumerate(parts):
        floors = ceils = None
        for s in range(S):
            right = enc_r[s, :, p]
            for left_floor, left_ceil in lefts[s]:
                df, dc = dot(left_floor, right), dot(left_ceil, right)
                floors = df if floors is None else jnp.maximum(floors, df)
                ceils = dc if ceils is None else jnp.maximum(ceils, dc)
        old = w[:, p]
        new = jnp.minimum(old.astype(F32), decode(floors, ceils, 2.0)).astype(jnp.int32)
        lag = lax.broadcasted_iota(jnp.int32, old.shape, 1) - lax.broadcasted_iota(jnp.int32, old.shape, 0)
        o[:, p] = jnp.where(lag == row * w.shape[0] - col * w.shape[1] - j * wide, 0, new)
        stores[j].start()
    for store in stores:
        store.wait()


def per_device(weights):
    dma = pltpu.SemaphoreType.DMA
    vmem = pl.BlockSpec(memory_space=pltpu.VMEM)
    rows, cols = weights.shape
    closed, r0, r1 = pl.pallas_call(
        gather_kernel,
        out_shape=(
            jax.ShapeDtypeStruct((S, rows, B), BF16),
            jax.ShapeDtypeStruct((S, S, 32, 512), BF16),
            jax.ShapeDtypeStruct((S, S, 32, 512), BF16),
        ),
        in_specs=[vmem],
        out_specs=(vmem, vmem, vmem),
        scratch_shapes=[
            pltpu.VMEM((S, 2, 32, 512), BF16),
            pltpu.VMEM((S, S, B, B), BF16),
            pltpu.VMEM((S, rows, B), BF16),
            pltpu.VMEM((2, 1024, 2 * B), F32),
            pltpu.VMEM((2, 2, 2 * B, 2 * B), BF16),
            dma((S,)), dma, dma((16,)), dma((16,)), dma((16,)), dma((S,)), dma((S,)), dma((S,)),
            dma((S,)), dma, dma((S,)), dma,
            dma((S,)), dma((S,)), dma((S,)), dma((S,)), dma((S,)), dma((S,)), dma((S,)), dma((S,)),
        ],
        compiler_params=pltpu.CompilerParams(
            collective_id=0, has_side_effects=True, vmem_limit_bytes=24 * 2**20
        ),
        name="gather",
    )(weights)
    return pl.pallas_call(
        product_kernel,
        out_shape=jax.ShapeDtypeStruct(weights.shape, jnp.int32),
        in_specs=[vmem] * 4,
        out_specs=pl.BlockSpec(memory_space=pltpu.HBM),
        scratch_shapes=[
            pltpu.VMEM((rows, cols), jnp.int32),
            pltpu.VMEM((S, 2 * B, cols), BF16),
            dma((4,)),
        ],
        compiler_params=pltpu.CompilerParams(vmem_limit_bytes=32 * 2**20),
        name="product",
    )(weights, closed, r0, r1)


def solution(mesh):
    return jax.shard_map(
        per_device, mesh=mesh, in_specs=(P("row", "col"),), out_specs=P("row", "col"), check_vma=False
    )
```

time: 45.2 us -> 38 us (0.84)
  Pallas kernels: 43.3 us -> 36.1 us
    pallas_call x1, Pallas kernels: 11 us -> 7.11 us  [per_device(): pl.pallas_call(product_kernel, out_shape=jax.ShapeDtypeStruct(weights.sha...]
    pallas_call x1, Pallas kernels: 32.3 us -> 28.9 us  [per_device(): pl.pallas_call(gather_kernel, out_shape=(jax.ShapeDtypeStruct((S, rows, B...]
    unnamed x2 -> x4, local copies, waits for them, and re-layouts: 1.59 us -> 1.59 us
where the time goes in v3:
time: 38 us; the launch traced here: 37.8 us
  Pallas kernels  36.1 us (95%)
  local copies, waits for them, and re-layouts  1.59 us (4%)
    pallas_call x1, Pallas kernels, per_device(): pl.pallas_call(gather_kernel, out_shape=(jax.ShapeDtypeStruct((S, rows, B...  28.9 us
    pallas_call x1, Pallas kernels, per_device(): pl.pallas_call(product_kernel, out_shape=jax.ShapeDtypeStruct(weights.sha...  7.11 us
    unnamed x4, local copies, waits for them, and re-layouts  1.59 us

profile of v3, /device:TPU:1, one launch (start us, length us, event | category | flops | bytes accessed | tf_op | source)
XLA Modules:
  0.0 37.8 jit_solution(11805908952344937670)
XLA Ops:
  0.0 0.0 copy-start
  0.0 1.6 %copy-done = s32[512,1024]{1,0:T(8,128)S(1)} copy-done((s32[512,1024]{1,0:T(8,128)S(1)}, s32[512,1024]{1,0:T(8,128)}, u32[]{:S(2)}) %copy-start) | copy-done | bytes 2097176
  1.6 0.0 copy-start.1
  1.6 28.9 %gather.1 = (bf16[4,512,128]{2,1,0:T(8,128)(2,1)S(1)}, bf16[4,4,32,512]{3,2,1,0:T(8,128)(2,1)S(1)}, bf16[4,4,32,512]{3,2,1,0:T(8,128)(2,1)S(1)}) custom-call(s32[512,1024]{1,0:T(8,128)S(1)} %copy-done), custom_call_target="tpu_custom_call" | custom-call | tf_op jit(solution)/shard_map/gather/pallas_call | solution.py:380
  30.6 0.0 copy-done.1
  30.6 7.1 %product.1 = s32[512,1024]{1,0:T(8,128)} custom-call(s32[512,1024]{1,0:T(8,128)S(1)} %copy-done.1, bf16[4,512,128]{2,1,0:T(8,128)(2,1)S(1)} %get-tuple-element.8.x_ref, bf16[4,4,32,512]{3,2,1,0:T(8,128)(2,1)S(1)} %get-tuple-element.9.r0, bf16[4,4,32,512]{3,2,1,0:T(8,128)(2,1)S(1)} %get-tuple-element.10.r1), custom_call_target="tpu_custom_call" | custom-call | tf_op jit(solution)/shard_map/product/pallas_call | solution.py:404
Async XLA Ops:
  0.0 1.6 %copy-start = (s32[512,1024]{1,0:T(8,128)S(1)}, s32[512,1024]{1,0:T(8,128)}, u32[]{:S(2)}) copy-start(s32[512,1024]{1,0:T(8,128)} %w.3) | copy-start | bytes 6291460
  1.6 29.0 %copy-start.1 = (s32[512,1024]{1,0:T(8,128)S(1)}, s32[512,1024]{1,0:T(8,128)}, u32[]{:S(2)}) copy-start(s32[512,1024]{1,0:T(8,128)} %w.3) | copy-start | bytes 6291460

commit v4 on v3

--- a/solution.py
+++ b/solution.py
@@ -87,8 +87,8 @@
 
 
 def gather_kernel(
-    w, x_ref, r0, r1, rs, yp, yi, y, enc_row,
-    p1_send, p1_recv, p2_send, p2_recv, pf_send, yi_send, yi_recv, fi_send,
+    w_hbm, x_ref, r0, r1, wp, wr, wc, rs, yp, yi, y, enc_row,
+    w_sem, p1_send, p1_recv, p2_send, p2_recv, pf_send, yi_send, yi_recv, fi_send,
     s0_send, s0_recv, s1_send, s1_recv, a0_send, a0_recv, a1_send, a1_recv, b0_send, b0_recv, b1_send, b1_recv,
 ):
     row, col = lax.axis_index("row"), lax.axis_index("col")
@@ -120,21 +120,26 @@
         greet(in_slab(d)[2])
     greet(partner)
 
+    load_block = pltpu.make_async_copy(w_hbm.at[pl.ds(0, B), pl.ds(0, B)], wp, w_sem.at[0])
+    load_rows = pltpu.make_async_copy(w_hbm.at[pl.ds(0, B)], wr, w_sem.at[1])
+    load_cols = pltpu.make_async_copy(w_hbm.at[:, pl.ds(0, B)], wc, w_sem.at[2])
+
     @pl.when(block_owner)
     def _():
-        yp[cz, cx] = w[0:B, 0:B].astype(BF16)
+        load_block.start()
+
+    @pl.when(cy == 0)
+    def _():
+        load_rows.start()
 
     @pl.when(core == 0)
     def _():
-        yi[cz] = w[:, 0:B].astype(BF16)
-
-    @pl.when(cy == 0)
-    def _():
-        for q in range(S):
-            for h in range(2):
-                rs[q, h] = w[q * 32 : (q + 1) * 32, h * 512 : (h + 1) * 512].astype(BF16)
-        r0[0, cx] = w[0:32, 0:512].astype(BF16)
-        r1[cx, 0] = w[0:32, 512:1024].astype(BF16)
+        load_cols.start()
+
+    @pl.when(block_owner)
+    def _():
+        load_block.wait()
+        yp[cz, cx] = wp[...].astype(BF16)
 
     pl.semaphore_wait(barrier, 19)
 
@@ -200,6 +205,20 @@
     def _():
         for d in range(1, S):
             block_y(d).start()
+
+    @pl.when(core == 0)
+    def _():
+        load_cols.wait()
+        yi[cz] = wc[...].astype(BF16)
+
+    @pl.when(cy == 0)
+    def _():
+        load_rows.wait()
+        for q in range(S):
+            for h in range(2):
+                rs[q, h] = wr[q * 32 : (q + 1) * 32, h * 512 : (h + 1) * 512].astype(BF16)
+        r0[0, cx] = wr[0:32, 0:512].astype(BF16)
+        r1[cx, 0] = wr[0:32, 512:1024].astype(BF16)
 
     @pl.when(core == 0)
     def _():
@@ -355,15 +374,18 @@
         return 0
 
     lax.fori_loop(0, S, encode_strip, 0)
-    lefts = [enc_left(x_ref[s].astype(F32)) for s in range(S)]
+    lefts = []
+    for s in range(S):
+        (f0, c0), (f1, c1) = enc_left(x_ref[s].astype(F32))
+        lefts.append((f0, f1, c0, c1))
     for j, p in enumerate(parts):
         floors = ceils = None
         for s in range(S):
             right = enc_r[s, :, p]
-            for left_floor, left_ceil in lefts[s]:
-                df, dc = dot(left_floor, right), dot(left_ceil, right)
-                floors = df if floors is None else jnp.maximum(floors, df)
-                ceils = dc if ceils is None else jnp.maximum(ceils, dc)
+            f0, f1, c0, c1 = (dot(left, right) for left in lefts[s])
+            df, dc = jnp.maximum(f0, f1), jnp.maximum(c0, c1)
+            floors = df if floors is None else jnp.maximum(floors, df)
+            ceils = dc if ceils is None else jnp.maximum(ceils, dc)
         old = w[:, p]
         new = jnp.minimum(old.astype(F32), decode(floors, ceils, 2.0)).astype(jnp.int32)
         lag = lax.broadcasted_iota(jnp.int32, old.shape, 1) - lax.broadcasted_iota(jnp.int32, old.shape, 0)
@@ -384,15 +406,18 @@
             jax.ShapeDtypeStruct((S, S, 32, 512), BF16),
             jax.ShapeDtypeStruct((S, S, 32, 512), BF16),
         ),
-        in_specs=[vmem],
+        in_specs=[pl.BlockSpec(memory_space=pltpu.HBM)],
         out_specs=(vmem, vmem, vmem),
         scratch_shapes=[
+            pltpu.VMEM((B, B), jnp.int32),
+            pltpu.VMEM((B, cols), jnp.int32),
+            pltpu.VMEM((rows, B), jnp.int32),
             pltpu.VMEM((S, 2, 32, 512), BF16),
             pltpu.VMEM((S, S, B, B), BF16),
             pltpu.VMEM((S, rows, B), BF16),
             pltpu.VMEM((2, 1024, 2 * B), F32),
             pltpu.VMEM((2, 2, 2 * B, 2 * B), BF16),
-            dma((S,)), dma, dma((16,)), dma((16,)), dma((16,)), dma((S,)), dma((S,)), dma((S,)),
+            dma((3,)), dma((S,)), dma, dma((16,)), dma((16,)), dma((16,)), dma((S,)), dma((S,)), dma((S,)),
             dma((S,)), dma, dma((S,)), dma,
             dma((S,)), dma((S,)), dma((S,)), dma((S,)), dma((S,)), dma((S,)), dma((S,)), dma((S,)),
         ],
@@ -400,7 +425,7 @@
             collective_id=0, has_side_effects=True, vmem_limit_bytes=24 * 2**20
         ),
         name="gather",
-    )(weights)
+    )(pltpu.with_memory_space_constraint(weights, pltpu.HBM))
     return pl.pallas_call(
         product_kernel,
         out_shape=jax.ShapeDtypeStruct(weights.shape, jnp.int32),

time: 38 us -> 36.3 us (0.955)
  local copies, waits for them, and re-layouts: 1.59 us -> 0.01 us
    unnamed x4 -> x2, local copies, waits for them, and re-layouts: 1.59 us -> 0.01 us
where the time goes in v4:
time: 36.3 us; the launch traced here: 36.1 us
  Pallas kernels  36 us (99%)
    pallas_call x1, Pallas kernels, per_device(): pl.pallas_call(gather_kernel, out_shape=(jax.ShapeDtypeStruct((S, rows, B...  29.1 us
    pallas_call x1, Pallas kernels, per_device(): pl.pallas_call(product_kernel, out_shape=jax.ShapeDtypeStruct(weights.sha...  6.84 us

profile of v4, /device:TPU:1, one launch (start us, length us, event | category | flops | bytes accessed | tf_op | source)
XLA Modules:
  0.0 36.1 jit_solution(14585521629131030425)
XLA Ops:
  0.0 0.0 copy-start
  0.0 29.1 %gather.1 = (bf16[4,512,128]{2,1,0:T(8,128)(2,1)S(1)}, bf16[4,4,32,512]{3,2,1,0:T(8,128)(2,1)S(1)}, bf16[4,4,32,512]{3,2,1,0:T(8,128)(2,1)S(1)}) custom-call(s32[512,1024]{1,0:T(8,128)} %w.1), custom_call_target="tpu_custom_call" | custom-call | tf_op jit(solution)/shard_map/gather/pallas_call | solution.py:402
  29.1 0.0 copy-done
  29.1 6.8 %product.1 = s32[512,1024]{1,0:T(8,128)} custom-call(s32[512,1024]{1,0:T(8,128)S(1)} %copy-done, bf16[4,512,128]{2,1,0:T(8,128)(2,1)S(1)} %get-tuple-element.8.x_ref, bf16[4,4,32,512]{3,2,1,0:T(8,128)(2,1)S(1)} %get-tuple-element.9.r0, bf16[4,4,32,512]{3,2,1,0:T(8,128)(2,1)S(1)} %get-tuple-element.10.r1), custom_call_target="tpu_custom_call" | custom-call | tf_op jit(solution)/shard_map/product/pallas_call | solution.py:429
Async XLA Ops:
  0.0 29.1 %copy-start = (s32[512,1024]{1,0:T(8,128)S(1)}, s32[512,1024]{1,0:T(8,128)}, u32[]{:S(2)}) copy-start(s32[512,1024]{1,0:T(8,128)} %w.1) | copy-start | bytes 6291460

commit v5 on v4

--- a/solution.py
+++ b/solution.py
@@ -193,13 +193,11 @@
             for copy in stage_a(d, cx, cy):
                 copy.start()
 
-    def start_b():
-        for d in range(1, S):
-            for copy in stage_a(d, (cx + d) % S, (cy + d) % S):
-                copy.wait_recv()
-        for d in range(1, S):
-            for copy in stage_b(d, cx, cy):
-                copy.start()
+    def start_b(half):
+        for d in range(1, S):
+            stage_a(d, (cx + d) % S, (cy + d) % S)[half].wait_recv()
+        for d in range(1, S):
+            stage_b(d, cx, cy)[half].start()
 
     @pl.when(block_owner)
     def _():
@@ -285,6 +283,8 @@
             enc_row[s % 2, u, 0:B, :] = ceil
             enc_row[s % 2, u, B : 2 * B, :] = floor
 
+    start_b(0)
+
     @pl.when(here != 0)
     def _():
         take((16 - here) % 16)
@@ -296,7 +296,7 @@
         return block
 
     block = lax.fori_loop(0, 5, square_and_take, yp[0, 0].astype(F32) - 1.0)
-    start_b()
+    start_b(1)
     block = min_plus_block(block)
 
     for t in range(S):
@@ -359,21 +359,17 @@
           copy.wait_send()
 
 
-def product_kernel(w, x_ref, r0, r1, o_hbm, o, enc_r, o_sem):
+def product_kernel(w, x_ref, r0, r1, o_hbm, o, o_sem):
     row, col = lax.axis_index("row"), lax.axis_index("col")
     wide = 2 * B
     parts = [pl.ds(j * wide, wide) for j in range(w.shape[1] // wide)]
     stores = [pltpu.make_async_copy(o.at[:, p], o_hbm.at[:, p], o_sem.at[j]) for j, p in enumerate(parts)]
 
-    def encode_strip(s, _):
-        for q in range(S):
-            for h, part in ((0, r0[q, s]), (1, r1[s, q])):
-                ceil, floor = enc_right(part.astype(F32) - 1.0)
-                enc_r[s, q * 32 : (q + 1) * 32, h * 512 : (h + 1) * 512] = ceil
-                enc_r[s, B + q * 32 : B + (q + 1) * 32, h * 512 : (h + 1) * 512] = floor
-        return 0
-
-    lax.fori_loop(0, S, encode_strip, 0)
+    def right_operand(s, j):
+        lanes = pl.ds(j % 2 * wide, wide)
+        quarters = [(r0[q, s, :, lanes] if j < 2 else r1[s, q, :, lanes]) for q in range(S)]
+        return jnp.concatenate(enc_right(jnp.concatenate(quarters, 0).astype(F32) - 1.0), 0)
+
     lefts = []
     for s in range(S):
         (f0, c0), (f1, c1) = enc_left(x_ref[s].astype(F32))
@@ -381,7 +377,7 @@
     for j, p in enumerate(parts):
         floors = ceils = None
         for s in range(S):
-            right = enc_r[s, :, p]
+            right = right_operand(s, j)
             f0, f1, c0, c1 = (dot(left, right) for left in lefts[s])
             df, dc = jnp.maximum(f0, f1), jnp.maximum(c0, c1)
             floors = df if floors is None else jnp.maximum(floors, df)
@@ -433,7 +429,6 @@
         out_specs=pl.BlockSpec(memory_space=pltpu.HBM),
         scratch_shapes=[
             pltpu.VMEM((rows, cols), jnp.int32),
-            pltpu.VMEM((S, 2 * B, cols), BF16),
             dma((4,)),
         ],
         compiler_params=pltpu.CompilerParams(vmem_limit_bytes=32 * 2**20),

time: 36.3 us -> 35.1 us (0.967)
  Pallas kernels: 36 us -> 34.7 us
    pallas_call x1, Pallas kernels: 29.1 us -> 28.4 us  [per_device(): pl.pallas_call(gather_kernel, out_shape=(jax.ShapeDtypeStruct((S, rows, B...]
    pallas_call x1, Pallas kernels: 6.84 us -> 6.26 us  [per_device(): pl.pallas_call(product_kernel, out_shape=jax.ShapeDtypeStruct(weights.sha...]
where the time goes in v5:
time: 35.1 us; the launch traced here: 34.7 us
  Pallas kernels  34.7 us (99%)
    pallas_call x1, Pallas kernels, per_device(): pl.pallas_call(gather_kernel, out_shape=(jax.ShapeDtypeStruct((S, rows, B...  28.4 us
    pallas_call x1, Pallas kernels, per_device(): pl.pallas_call(product_kernel, out_shape=jax.ShapeDtypeStruct(weights.sha...  6.26 us

profile of v5, /device:TPU:1, one launch (start us, length us, event | category | flops | bytes accessed | tf_op | source)
XLA Modules:
  0.0 34.7 jit_solution(16513551214867684581)
XLA Ops:
  0.0 0.0 copy-start
  0.0 28.4 %gather.1 = (bf16[4,512,128]{2,1,0:T(8,128)(2,1)S(1)}, bf16[4,4,32,512]{3,2,1,0:T(8,128)(2,1)S(1)}, bf16[4,4,32,512]{3,2,1,0:T(8,128)(2,1)S(1)}) custom-call(s32[512,1024]{1,0:T(8,128)} %w.1), custom_call_target="tpu_custom_call" | custom-call | tf_op jit(solution)/shard_map/gather/pallas_call | solution.py:398
  28.4 0.0 copy-done
  28.5 6.3 %product.1 = s32[512,1024]{1,0:T(8,128)} custom-call(s32[512,1024]{1,0:T(8,128)S(1)} %copy-done, bf16[4,512,128]{2,1,0:T(8,128)(2,1)S(1)} %get-tuple-element.8.x_ref, bf16[4,4,32,512]{3,2,1,0:T(8,128)(2,1)S(1)} %get-tuple-element.9.r0, bf16[4,4,32,512]{3,2,1,0:T(8,128)(2,1)S(1)} %get-tuple-element.10.r1), custom_call_target="tpu_custom_call" | custom-call | tf_op jit(solution)/shard_map/product/pallas_call | solution.py:425
Async XLA Ops:
  0.0 28.4 %copy-start = (s32[512,1024]{1,0:T(8,128)S(1)}, s32[512,1024]{1,0:T(8,128)}, u32[]{:S(2)}) copy-start(s32[512,1024]{1,0:T(8,128)} %w.1) | copy-start | bytes 6291460
